TPU v7x, 32 devices: a whole 2x2x4 slice. The times are simulated.
32 devices in a mesh: band: 8 (over z, y), grid: 4 (over x, core).
Axes of the slice: x: 2, y: 2, z: 4, core: 2. Of those that a mesh axis runs over, the one named last changes fastest.
Arguments:
- own_bands: float32 [32, 128, 128, 128], P('band', 'grid'), may hold values from -1.5 to 1.5
- travel_bands: float32 [32, 128, 128, 128], P('band', 'grid'), may hold values from -1.5 to 1.5
Outputs:
- own_terms: float32 [32, 128, 128, 128], P('band', 'grid')
- partner_terms: float32 [32, 128, 128, 128], P('band', 'grid')
All inputs are finite; a program needn't handle non-finite values.
Results may differ from a plain program's by a relative error of at most 0.00011.
Values sent between devices are 32-bit elements; how exact they have to be, the bound alone decides.
No kernel may reach another device: no remote copies, remote signals or barrier semaphores. Data moves between devices by JAX's collectives and lax.ppermute only.
A program may use at most 192 MiB of HBM per device.

v0:
```python
import math, functools
import numpy as np
import jax
import jax.numpy as jnp
from jax import lax
from jax.experimental import pallas as pl
from jax.experimental.pallas import tpu as pltpu
import ml_dtypes
BF = jnp.bfloat16
F32 = jnp.float32


def split_table(t):
    hi = t.astype(np.float32).astype(ml_dtypes.bfloat16)
    lo = (t - hi.astype(np.float64)).astype(np.float32).astype(ml_dtypes.bfloat16)
    return hi, lo


def dft(length, inverse):
    k = np.arange(length)
    ang = 2.0 * np.pi / length * ((k[:, None] * k[None, :]) % length)
    c, s = np.cos(ang), np.sin(ang)
    if inverse:
        s = -s
    return np.block([[c, s], [-s, c]])


def left_table(length, inverse):
    hi, lo = split_table(dft(length, inverse))
    return np.concatenate([hi, hi, lo], axis=1)


def right_table(length, inverse):
    hi, lo = split_table(dft(length, inverse).T)
    return np.concatenate([hi, hi, lo], axis=0)


def parts(v):
    hi = v.astype(BF)
    lo = (v - hi.astype(F32)).astype(BF)
    return hi, lo


def fft_body(*refs, n, pz, py, chunk, pitch, accumulate, n_own, four_pi, pieces, zchunk, lag):
    nz, ny, nx = n
    q_ref, own_ref = refs[:2]
    a, b = pieces
    vis_refs = refs[2:2 + a * b]
    rest = list(refs[2 + a * b:])
    prev_ref = rest.pop(0) if accumulate else None
    lyf, lyi, rxf, rxi, lzf, lzi, own_out, part_out, re_s, im_s, st_l, st_r, st_z2, ksq, vis_ref = rest
    st_z = st_l
    step = pl.program_id(0)
    na = nz // pz
    nb = ny // py

    def put_left(st, a, j, w, re, im):
        rh, rl = parts(re); ih, il = parts(im)
        col = slice(j * w, (j + 1) * w)
        st[0 * a:1 * a, col] = rh
        st[1 * a:2 * a, col] = ih
        st[2 * a:3 * a, col] = rl
        st[3 * a:4 * a, col] = il

    def put_right(st, a, w, j, re, im):
        rh, rl = parts(re); ih, il = parts(im)
        row = slice(j * a, (j + 1) * a)
        st[row, 0 * w:1 * w] = rh
        st[row, 1 * w:2 * w] = ih
        st[row, 2 * w:3 * w] = rl
        st[row, 3 * w:4 * w] = il

    def left(st, a, lo, hi):
        return jnp.concatenate([st[:4 * a, lo:hi], st[:2 * a, lo:hi]], axis=0)

    def right(st, w, lo, hi):
        return jnp.concatenate([st[lo:hi, :], st[lo:hi, :2 * w]], axis=1)

    def dot(a, b):
        return lax.dot_general(a, b, (((1,), (0,)), ((), ())), preferred_element_type=F32)

    def pipeline(first, second, third, count, width):
        n = count // width
        for t in range(n + 2 * lag):
            if t < n:
                first(t * width)
            if 0 <= t - lag < n:
                second((t - lag) * width)
            if 0 <= t - 2 * lag < n:
                third((t - 2 * lag) * width)

    plane = jnp.where(step < na, step, step - na - nb)
    natural = plane // (na // (a * b))
    for dx in range(a):
        for dc in range(b):
            here = ((q_ref[0] + dx) % a) * b + (q_ref[1] + dc) % b

            @pl.when(((step < na) | (step >= na + nb)) & (natural == here))
            def _(dx=dx, dc=dc):
                vis_ref[...] = vis_refs[dx * b + dc][0]

    @pl.when(step < na)
    def _():
        z0 = step * pz

        def density(c0):
            for p in range(c0, c0 + chunk):
                v = vis_ref[p]
                re = own_ref[0, 0, p] * v
                im = own_ref[0, 1, p] * v if n_own == 2 else jnp.zeros_like(re)
                put_left(st_l, ny, p, nx, re, im)

        def yforward(c0):
            y1 = dot(lyf[...], left(st_l, ny, c0 * nx, (c0 + chunk) * nx))
            for p in range(c0, c0 + chunk):
                j = p - c0
                put_right(st_r, ny, nx, p, y1[:ny, j * nx:(j + 1) * nx], y1[ny:, j * nx:(j + 1) * nx])

        def xforward(c0):
            y2 = dot(right(st_r, nx, c0 * ny, (c0 + chunk) * ny), rxf[...])
            for p in range(c0, c0 + chunk):
                j = p - c0
                row = pl.multiple_of((z0 + p) * pitch, 8)
                re_s[pl.ds(row, ny), :] = y2[j * ny:(j + 1) * ny, :nx]
                im_s[pl.ds(row, ny), :] = y2[j * ny:(j + 1) * ny, nx:]

        pipeline(density, yforward, xforward, pz, chunk)

    def square(i, length):
        pos = jnp.where(i >= length // 2, i - length, i).astype(F32) * F32(2.0 * math.pi / length)
        return pos * pos

    @pl.when(step == na)
    def _():
        iz = lax.broadcasted_iota(jnp.int32, (nz, nx), 0)
        ix = lax.broadcasted_iota(jnp.int32, (nz, nx), 1)
        ksq[...] = square(iz, nz) + square(ix, nx)

    @pl.when((step >= na) & (step < na + nb))
    def _():
        y0 = (step - na) * py

        def zload(c0):
            for j in range(c0, c0 + zchunk):
                re = re_s[pl.ds(y0 + j, nz, stride=pitch), :]
                im = im_s[pl.ds(y0 + j, nz, stride=pitch), :]
                put_left(st_z, nz, j, nx, re, im)

        def zforward(c0):
            f = dot(lzf[...], left(st_z, nz, c0 * nx, (c0 + zchunk) * nx))
            for j in range(c0, c0 + zchunk):
                k2 = ksq[...] + square(y0 + j, ny)
                kern = jnp.where(k2 > 0.0, F32(four_pi) / jnp.where(k2 > 0.0, k2, 1.0), 0.0)
                i = j - c0
                put_left(st_z2, nz, j, nx, f[:nz, i * nx:(i + 1) * nx] * kern, f[nz:, i * nx:(i + 1) * nx] * kern)

        def zinverse(c0):
            g = dot(lzi[...], left(st_z2, nz, c0 * nx, (c0 + zchunk) * nx))
            for j in range(c0, c0 + zchunk):
                i = j - c0
                re_s[pl.ds(y0 + j, nz, stride=pitch), :] = g[:nz, i * nx:(i + 1) * nx]
                im_s[pl.ds(y0 + j, nz, stride=pitch), :] = g[nz:, i * nx:(i + 1) * nx]

        pipeline(zload, zforward, zinverse, py, zchunk)

    @pl.when(step >= na + nb)
    def _():
        z0 = (step - na - nb) * pz

        def spectrum(c0):
            for p in range(c0, c0 + chunk):
                row = pl.multiple_of((z0 + p) * pitch, 8)
                put_right(st_r, ny, nx, p, re_s[pl.ds(row, ny), :], im_s[pl.ds(row, ny), :])

        def xinverse(c0):
            y2 = dot(right(st_r, nx, c0 * ny, (c0 + chunk) * ny), rxi[...])
            for p in range(c0, c0 + chunk):
                j = p - c0
                put_left(st_l, ny, p, nx, y2[j * ny:(j + 1) * ny, :nx], y2[j * ny:(j + 1) * ny, nx:])

        def yinverse(c0):
            y1 = dot(lyi[...], left(st_l, ny, c0 * nx, (c0 + chunk) * nx))
            for p in range(c0, c0 + chunk):
                j = p - c0
                v = vis_ref[p]
                va = y1[:ny, j * nx:(j + 1) * nx]
                o = va * v
                own_out[0, 0, p] = o + prev_ref[0, 0, p] if accumulate else o
                pt = va * own_ref[0, 0, p]
                if n_own == 2:
                    vb = y1[ny:, j * nx:(j + 1) * nx]
                    o = vb * v
                    own_out[0, 1, p] = o + prev_ref[0, 1, p] if accumulate else o
                    pt = pt + vb * own_ref[0, 1, p]
                part_out[0, p] = pt

        pipeline(spectrum, xinverse, yinverse, pz, chunk)


def solve(q, own, vis, prev, pieces, scale, pz=8, py=8, chunk=2, pad=8, zchunk=None, lag=1):
    _, n_own, planes, ny, nx = own.shape
    a, b = pieces
    nz = planes * a * b
    na, nb = nz // pz, ny // py
    per = planes // pz

    def zblk(i, q):
        t = jnp.where(i < na, i, jnp.maximum(i - nb, na) - na)
        t = jnp.where((i >= na) & (i < na + nb), na - 1, t)
        piece = t // per
        x, c = piece // b, piece % b
        rel = ((x - q[0] + a) % a) * b + (c - q[1] + b) % b
        return rel, t % per

    def zout(i, q):
        t = jnp.maximum(i - nb - na, 0)
        piece = t // per
        x, c = piece // b, piece % b
        rel = ((x - q[0] + a) % a) * b + (c - q[1] + b) % b
        return rel, t % per

    def vis_blk(i, q, dx, dc, many):
        t = jnp.where(i < na + nb, jnp.minimum(i, na - 1), i - na - nb)
        here = ((q[0] + dx) % a) * b + (q[1] + dc) % b
        return (q[1] if many else 0, jnp.clip(t - here * per, 0, per - 1), 0, 0)

    own_in = pl.BlockSpec((1, n_own, pz, ny, nx), lambda i, q: (zblk(i, q)[0], 0, zblk(i, q)[1], 0, 0))
    vis_in = [
        pl.BlockSpec((1, pz, ny, nx), functools.partial(vis_blk, dx=r // b, dc=r % b, many=vis[r].shape[0] > 1))
        for r in range(a * b)
    ]
    prev_in = pl.BlockSpec((1, n_own, pz, ny, nx), lambda i, q: (zout(i, q)[0], 0, zout(i, q)[1], 0, 0))
    own_o = pl.BlockSpec((1, n_own, pz, ny, nx), lambda i, q: (zout(i, q)[0], 0, zout(i, q)[1], 0, 0))
    part_o = pl.BlockSpec((1, pz, ny, nx), lambda i, q: (zout(i, q)[0], zout(i, q)[1], 0, 0))
    tabs = [left_table(ny, False), left_table(ny, True), right_table(nx, False), right_table(nx, True), left_table(nz, False), left_table(nz, True)]
    tab_specs = [pl.BlockSpec(t.shape, lambda i, q: (0, 0), pipeline_mode=pl.Buffered(1)) for t in tabs]
    pitch = ny + pad
    body = functools.partial(fft_body, n=(nz, ny, nx), pz=pz, py=py, chunk=chunk, pitch=pitch, accumulate=prev is not None, n_own=n_own, four_pi=scale, pieces=pieces, zchunk=zchunk or chunk, lag=lag)
    ins = [own] + list(vis) + ([prev] if prev is not None else []) + [jnp.asarray(t) for t in tabs]
    specs = [own_in] + vis_in + ([prev_in] if prev is not None else []) + tab_specs
    flops = 6 * 3 * 2 * nz * ny * 4 * nx * nx
    return pl.pallas_call(
        body,
        grid_spec=pltpu.PrefetchScalarGridSpec(
            num_scalar_prefetch=1, grid=(2 * na + nb,), in_specs=specs, out_specs=[own_o, part_o],
            scratch_shapes=[pltpu.VMEM((nz * pitch, nx), F32), pltpu.VMEM((nz * pitch, nx), F32),
                            pltpu.VMEM((4 * max(ny, nz), max(pz, py) * nx), BF), pltpu.VMEM((pz * ny, 4 * nx), BF),
                            pltpu.VMEM((4 * nz, py * nx), BF), pltpu.VMEM((nz, nx), F32),
                            pltpu.VMEM((pz, ny, nx), F32)]),
        out_shape=[jax.ShapeDtypeStruct(own.shape, F32), jax.ShapeDtypeStruct((a * b, planes, ny, nx), F32)],
        compiler_params=pltpu.CompilerParams(vmem_limit_bytes=58 * 2**20),
        cost_estimate=pl.CostEstimate(flops=flops, bytes_accessed=64 * 2**20, transcendentals=0),
    )(q, *ins)


from jax.sharding import PartitionSpec as P

FRACTION = 0.25


def factors(size, own, vis):
    pairs = [(a, size // a) for a in range(1, size + 1) if size % a == 0]
    return min((p for p in pairs if own % p[0] == 0 and vis % p[1] == 0), key=lambda p: abs(p[0] - p[1]))


def from_slow(block, a, b, shift):
    if shift == 0:
        return block
    return lax.ppermute(block, "grid", [(((x + shift) % a) * b + c, x * b + c) for x in range(a) for c in range(b)])


def from_fast(block, a, b, shift):
    if shift == 0:
        return block
    return lax.ppermute(block, "grid", [(x * b + (c + shift) % b, x * b + c) for x in range(a) for c in range(b)])


def along_band(block, distance):
    size = lax.axis_size("band")
    return lax.ppermute(block, "band", [((i - distance) % size, i) for i in range(size)])


def body(own_bands, travel_bands):
    own_count, planes, ny, nx = own_bands.shape
    vis_count = travel_bands.shape[0]
    size = lax.axis_size("grid")
    a, b = factors(size, own_count, vis_count)
    n_own, n_vis = own_count // a, vis_count // b
    nz = planes * size
    index = lax.axis_index("grid")
    x, c = index // b, index % b
    q = jnp.stack([x, c]).astype(jnp.int32)
    scale = -FRACTION * 4.0 * math.pi / (nz * ny * nx)
    pz = math.gcd(planes, 16)
    py = math.gcd(ny, 32)

    def own_set(bands, s):
        return lax.dynamic_slice_in_dim(bands, s * n_own, n_own, 0)

    arrived = [along_band(travel_bands[:b], 1)]
    sent = [own_set(own_bands, (x - dx) % a) for dx in range(1, a)]
    sent, own_bands, travel_bands = lax.optimization_barrier((sent, own_bands, travel_bands))
    own_x = [from_slow(s, a, b, dx + 1) for dx, s in enumerate(sent)]
    for k in range(1, n_vis):
        arrived.append(along_band(travel_bands[k * b:(k + 1) * b], 1))
    own_x = [own_set(own_bands, x)] + own_x
    own_full = jnp.stack([from_fast(own_x[dx], a, b, dc) for dx in range(a) for dc in range(b)])

    groups = [(g, min(2, n_own - g)) for g in range(0, n_own, 2)]
    own_part = [None for _ in groups]
    returned = []
    last = None
    for k in range(n_vis):
        pieces = [from_slow(arrived[k], a, b, dx) for dx in range(a)]
        vis = []
        for dx in range(a):
            vis.append(pieces[dx])
            for dc in range(1, b):
                vis.append(from_fast(lax.dynamic_slice_in_dim(pieces[dx], (c - dc) % b, 1, 0), a, b, dc))
        partner = None
        for n, (g, w) in enumerate(groups):
            own_part[n], part = solve(q, own_full[:, g:g + w], vis, own_part[n], (a, b), scale, pz=pz, py=py)
            partner = part if partner is None else partner + part
        partner = partner.reshape(a, b, planes, ny, nx)
        back = []
        for dc in range(b):
            here = [from_fast(partner[dx, dc], a, b, (-dc) % b) for dx in range(a)]
            got = [from_slow(here[dx], a, b, (-dx) % a) for dx in range(1, a)]
            if last is not None:
                got, last = lax.optimization_barrier((got, last))
                if dc:
                    back[-1] = last
                else:
                    returned[-1][-1] = last
            last = here[0]
            for piece in got:
                last = last + piece
            back.append(last)
        returned.append(back)

    own_part = own_part[0] if len(groups) == 1 else jnp.concatenate(own_part, axis=1)
    own_part = own_part.reshape(a, b, n_own, planes, ny, nx)
    for dx in range(a):
        summed = own_part[dx, 0]
        for dc in range(1, b):
            summed = summed + from_fast(own_part[dx, dc], a, b, (-dc) % b)
        if dx == 0:
            own_out = jnp.concatenate([summed] * a, axis=0)
            continue
        got = from_slow(summed, a, b, (-dx) % a)
        own_out = lax.dynamic_update_slice_in_dim(own_out, got, ((x - dx) % a) * n_own, 0)
    partner_out = jnp.zeros_like(travel_bands)
    for k in range(n_vis):
        for dc in range(b):
            got = along_band(returned[k][dc], -1)
            partner_out = lax.dynamic_update_index_in_dim(partner_out, got, k * b + (c - dc) % b, 0)
    return own_out, partner_out


def solution(mesh):
    spec = P("band", "grid", None, None)
    return jax.shard_map(body, mesh=mesh, in_specs=(spec, spec), out_specs=(spec, spec), check_vma=False)
```

profile of v0, /device:TPU:0, one launch (start us, length us, event | category | flops | bytes accessed | tf_op | source)
XLA Modules:
  0.0 743.0 jit_solution(7061250554290476456)
XLA Ops:
  0.6 4.7 slice.43
  8.3 5.0 constant_dynamic-slice_fusion.5
  19.8 83.3 %collective-permute-done.7.refs_2_ = f32[2,32,128,128]{3,2,1,0:T(8,128)} collective-permute-done((f32[2,32,128,128]{3,2,1,0:T(8,128)}, f32[2,32,128,128]{3,2,1,0:T(8,128)}, u32[]{:S(2)}, u32[]{:S(2)}) %collective-permute-start.7) | collective-permute-done | bytes 4194336 | tf_op jit(solution)/shard_map/ppermute | solution.py:280
  104.8 87.4 %collective-permute-done.3.refs_2_ = f32[2,32,128,128]{3,2,1,0:T(8,128)} collective-permute-done((f32[2,32,128,128]{3,2,1,0:T(8,128)}, f32[2,32,128,128]{3,2,1,0:T(8,128)}, u32[]{:S(2)}, u32[]{:S(2)}) %collective-permute-start.3) | collective-permute-done | bytes 4194336 | tf_op jit(solution)/shard_map/ppermute | solution.py:280
  193.6 4.7 constant_dynamic-slice_fusion.4
  208.7 81.4 %collective-permute-done.5.refs_4_ = f32[2,32,128,128]{3,2,1,0:T(8,128)} collective-permute-done((f32[2,32,128,128]{3,2,1,0:T(8,128)}, f32[2,32,128,128]{3,2,1,0:T(8,128)}, u32[]{:S(2)}, u32[]{:S(2)}) %collective-permute-start.5) | collective-permute-done | bytes 4194336 | tf_op jit(solution)/shard_map/ppermute | solution.py:269
  292.5 10.8 %pad_maximum_fusion.refs_1_ = f32[4,2,32,128,128]{4,3,2,1,0:T(8,128)} fusion(f32[1,2,32,128,128]{4,3,2,1,0:T(8,128)} %bitcast.5, f32[1,2,32,128,128]{4,3,2,1,0:T(8,128)} %bitcast.4, f32[1,2,32,128,128]{4,3,2,1,0:T(8,128)} %bitcast.3, f32[1,2,32,128,128]{4,3,2,1,0:T(8,128)S(1)} %fusion.4), kind=kLoop, calls=%fused_computation | loop fusion | flops 12582912 | bytes 33554432 | tf_op jit(solution)/shard_map/stack | solution.py:307
  304.7 66.4 %shard_map.149 = (f32[4,2,32,128,128]{4,3,2,1,0:T(8,128)}, f32[4,32,128,128]{3,2,1,0:T(8,128)}) custom-call(s32[2]{0:T(128)} %pad_add_fusion.refs_0_, f32[4,2,32,128,128]{4,3,2,1,0:T(8,128)} %pad_maximum_fusion.refs_1_, f32[2,32,128,128]{3,2,1,0:T(8,128)} %collective-permute-done.7.refs_2_, f32[1,32,128,128]{3,2,1,0:T(8,128)} %copy-done.7, ...), custom_call_target="tpu_custom_call" | custom-call | flops 38654705664 | bytes 67108864 | tf_op jit(solution)/shard_map/pallas_call | solution.py:242
  371.1 70.1 %shard_map.150 = (f32[4,2,32,128,128]{4,3,2,1,0:T(8,128)}, f32[4,32,128,128]{3,2,1,0:T(8,128)}) custom-call(s32[2]{0:T(128)} %pad_add_fusion.refs_0_, f32[4,2,32,128,128]{4,3,2,1,0:T(8,128)} %pad_maximum_fusion.refs_1_, f32[2,32,128,128]{3,2,1,0:T(8,128)} %collective-permute-done.3.refs_2_, f32[1,32,128,128]{3,2,1,0:T(8,128)} %collective-permute-done.4.refs_3_, ...), custom_call_target="tpu_custom_call" | custom-call | flops 38654705664 | bytes 67108864 | tf_op jit(solution)/shard_map/pallas_call | solution.py:242
  441.2 6.4 slice_bitcast_fusion
  455.6 8.6 %collective-permute-done.14 = f32[32,128,128]{2,1,0:T(8,128)} collective-permute-done((f32[32,128,128]{2,1,0:T(8,128)S(1)}, f32[32,128,128]{2,1,0:T(8,128)}, u32[]{:S(2)}, u32[]{:S(2)}) %collective-permute-start.14) | collective-permute-done | bytes 2097184 | tf_op jit(solution)/shard_map/ppermute | solution.py:275
  465.7 33.8 %collective-permute-done.16 = f32[32,128,128]{2,1,0:T(8,128)S(1)} collective-permute-done((f32[32,128,128]{2,1,0:T(8,128)}, f32[32,128,128]{2,1,0:T(8,128)S(1)}, u32[]{:S(2)}, u32[]{:S(2)}) %collective-permute-start.16) | collective-permute-done | bytes 2097184 | tf_op jit(solution)/shard_map/ppermute | solution.py:269
  502.4 10.2 %fusion = (f32[2,32,128,128]{3,2,1,0:T(8,128)}, f32[2,32,128,128]{3,2,1,0:T(8,128)}) fusion(f32[2,32,128,128]{3,2,1,0:T(8,128)} %collective-permute-done.12, f32[2,2,2,32,128,128]{5,4,3,2,1,0:T(8,128)} %bitcast.51, f32[2,32,128,128]{3,2,1,0:T(8,128)S(1)} %collective-permute-done.11), kind=kLoop, calls=%fused_computation.4 | loop fusion | flops 2097152 | bytes 25165824 | tf_op jit(solution)/shard_map/add | solution.py:346
  512.5 31.9 %collective-permute-done.15 = f32[32,128,128]{2,1,0:T(8,128)S(1)} collective-permute-done((f32[32,128,128]{2,1,0:T(8,128)}, f32[32,128,128]{2,1,0:T(8,128)S(1)}, u32[]{:S(2)}, u32[]{:S(2)}) %collective-permute-start.15) | collective-permute-done | bytes 2097184 | tf_op jit(solution)/shard_map/ppermute | solution.py:269
  549.9 3.3 collective-permute-start.17
  556.4 33.1 %collective-permute-done.18 = f32[32,128,128]{2,1,0:T(8,128)} collective-permute-done((f32[32,128,128]{2,1,0:T(8,128)}, f32[32,128,128]{2,1,0:T(8,128)}, u32[]{:S(2)}, u32[]{:S(2)}) %collective-permute-start.18) | collective-permute-done | bytes 2097184 | tf_op jit(solution)/shard_map/ppermute | solution.py:269
  592.7 3.9 fusion.2
  596.6 37.8 %collective-permute-done.22 = f32[32,128,128]{2,1,0:T(8,128)} collective-permute-done((f32[32,128,128]{2,1,0:T(8,128)}, f32[32,128,128]{2,1,0:T(8,128)}, u32[]{:S(2)}, u32[]{:S(2)}) %collective-permute-start.22) | collective-permute-done | bytes 2097184 | tf_op jit(solution)/shard_map/ppermute | solution.py:269
  637.6 3.9 add.91
  642.1 4.0 pad_maximum_fusion.1
  650.8 38.4 %collective-permute-done.23 = f32[32,128,128]{2,1,0:T(8,128)} collective-permute-done((f32[32,128,128]{2,1,0:T(8,128)}, f32[32,128,128]{2,1,0:T(8,128)}, u32[]{:S(2)}, u32[]{:S(2)}) %collective-permute-start.23) | collective-permute-done | bytes 2097184 | tf_op jit(solution)/shard_map/ppermute | solution.py:280
  691.0 41.1 %collective-permute-done.25 = f32[32,128,128]{2,1,0:T(8,128)} collective-permute-done((f32[32,128,128]{2,1,0:T(8,128)}, f32[32,128,128]{2,1,0:T(8,128)}, u32[]{:S(2)}, u32[]{:S(2)}) %collective-permute-start.25) | collective-permute-done | bytes 2097184 | tf_op jit(solution)/shard_map/ppermute | solution.py:280
  733.9 5.8 constant_dynamic-update-slice_fusion
  739.6 3.4 copy-done.1
  (77 shorter events, 62.8 us)
Async XLA Ops:
  5.3 97.8 %collective-permute-start.7 = (f32[2,32,128,128]{3,2,1,0:T(8,128)}, f32[2,32,128,128]{3,2,1,0:T(8,128)}, u32[]{:S(2)}, u32[]{:S(2)}) collective-permute-start(f32[2,32,128,128]{3,2,1,0:T(8,128)} %slice.43), channel_id=1, source_target_pairs={{28,0},{0,4},{4,8},{8,12},{12,16},{16,20},{20,24},{24,28},{29,1},{... | collective-permute-start | bytes 12582920 | tf_op jit(solution)/shard_map/ppermute | solution.py:280
  16.8 175.4 %collective-permute-start.3 = (f32[2,32,128,128]{3,2,1,0:T(8,128)}, f32[2,32,128,128]{3,2,1,0:T(8,128)}, u32[]{:S(2)}, u32[]{:S(2)}) collective-permute-start(f32[2,32,128,128]{3,2,1,0:T(8,128)} %slice.42), channel_id=1, source_target_pairs={{28,0},{0,4},{4,8},{8,12},{12,16},{16,20},{20,24},{24,28},{29,1},{... | collective-permute-start | bytes 12582920 | tf_op jit(solution)/shard_map/ppermute | solution.py:280
  18.3 180.0 %collective-permute-start.1 = (f32[2,32,128,128]{3,2,1,0:T(8,128)}, f32[2,32,128,128]{3,2,1,0:T(8,128)}, u32[]{:S(2)}, u32[]{:S(2)}) collective-permute-start(f32[2,32,128,128]{3,2,1,0:T(8,128)} %constant_dynamic-slice_fusion.5), channel_id=1, source_target_pairs={{2,0},{3,1},{0,2},{1,3},{6,4},{7,5},{4,6},{5,7},{10,8},{11,9},{8,1... | collective-permute-start | bytes 12582920 | tf_op jit(solution)/shard_map/ppermute | solution.py:269
  103.1 98.8 %collective-permute-start.9 = (f32[2,32,128,128]{3,2,1,0:T(8,128)}, f32[2,32,128,128]{3,2,1,0:T(8,128)}, u32[]{:S(2)}, u32[]{:S(2)}) collective-permute-start(f32[2,32,128,128]{3,2,1,0:T(8,128)} %collective-permute-done.7.refs_2_), channel_id=1, source_target_pairs={{2,0},{3,1},{0,2},{1,3},{6,4},{7,5},{4,6},{5,7},{10,8},{11,9},{8,1... | collective-permute-start | bytes 12582920 | tf_op jit(solution)/shard_map/ppermute | solution.py:269
  192.1 98.0 %collective-permute-start.5 = (f32[2,32,128,128]{3,2,1,0:T(8,128)}, f32[2,32,128,128]{3,2,1,0:T(8,128)}, u32[]{:S(2)}, u32[]{:S(2)}) collective-permute-start(f32[2,32,128,128]{3,2,1,0:T(8,128)} %collective-permute-done.3.refs_2_), channel_id=1, source_target_pairs={{2,0},{3,1},{0,2},{1,3},{6,4},{7,5},{4,6},{5,7},{10,8},{11,9},{8,1... | collective-permute-start | bytes 12582920 | tf_op jit(solution)/shard_map/ppermute | solution.py:269
  198.3 93.6 %collective-permute-start = (f32[2,32,128,128]{3,2,1,0:T(8,128)}, f32[2,32,128,128]{3,2,1,0:T(8,128)}, u32[]{:S(2)}, u32[]{:S(2)}) collective-permute-start(f32[2,32,128,128]{3,2,1,0:T(8,128)} %constant_dynamic-slice_fusion.4), channel_id=1, source_target_pairs={{1,0},{0,1},{3,2},{2,3},{5,4},{4,5},{7,6},{6,7},{9,8},{8,9},{11,10... | collective-permute-start | bytes 12582920 | tf_op jit(solution)/shard_map/ppermute | solution.py:275
  198.3 94.2 %collective-permute-start.2 = (f32[2,32,128,128]{3,2,1,0:T(8,128)}, f32[2,32,128,128]{3,2,1,0:T(8,128)}, u32[]{:S(2)}, u32[]{:S(2)}) collective-permute-start(f32[2,32,128,128]{3,2,1,0:T(8,128)} %collective-permute-done.1), channel_id=1, source_target_pairs={{1,0},{0,1},{3,2},{2,3},{5,4},{4,5},{7,6},{6,7},{9,8},{8,9},{11,10... | collective-permute-start | bytes 12582920 | tf_op jit(solution)/shard_map/ppermute | solution.py:275
  200.6 102.7 %collective-permute-start.8 = (f32[1,32,128,128]{3,2,1,0:T(8,128)S(1)}, f32[1,32,128,128]{3,2,1,0:T(8,128)S(1)}, u32[]{:S(2)}, u32[]{:S(2)}) collective-permute-start(f32[1,32,128,128]{3,2,1,0:T(8,128)S(1)} %constant_dynamic-slice_fusion.1), channel_id=1, source_target_pairs={{1,0},{0,1},{3,2},{2,3},{5,4},{4,5},{7,6},{6,7},{9,8},{8,9},{11,10... | collective-permute-start | bytes 6291464 | tf_op jit(solution)/shard_map/ppermute | solution.py:275
  203.7 101.0 %collective-permute-start.10 = (f32[1,32,128,128]{3,2,1,0:T(8,128)S(1)}, f32[1,32,128,128]{3,2,1,0:T(8,128)}, u32[]{:S(2)}, u32[]{:S(2)}) collective-permute-start(f32[1,32,128,128]{3,2,1,0:T(8,128)S(1)} %constant_dynamic-slice_fusion), channel_id=1, source_target_pairs={{1,0},{0,1},{3,2},{2,3},{5,4},{4,5},{7,6},{6,7},{9,8},{8,9},{11,10... | collective-permute-start | bytes 6291464 | tf_op jit(solution)/shard_map/ppermute | solution.py:275
  290.1 81.0 %collective-permute-start.4 = (f32[1,32,128,128]{3,2,1,0:T(8,128)S(1)}, f32[1,32,128,128]{3,2,1,0:T(8,128)}, u32[]{:S(2)}, u32[]{:S(2)}) collective-permute-start(f32[1,32,128,128]{3,2,1,0:T(8,128)S(1)} %constant_dynamic-slice_fusion.3), channel_id=1, source_target_pairs={{1,0},{0,1},{3,2},{2,3},{5,4},{4,5},{7,6},{6,7},{9,8},{8,9},{11,10... | collective-permute-start | bytes 6291464 | tf_op jit(solution)/shard_map/ppermute | solution.py:275
  292.0 79.1 %collective-permute-start.6 = (f32[1,32,128,128]{3,2,1,0:T(8,128)S(1)}, f32[1,32,128,128]{3,2,1,0:T(8,128)}, u32[]{:S(2)}, u32[]{:S(2)}) collective-permute-start(f32[1,32,128,128]{3,2,1,0:T(8,128)S(1)} %constant_dynamic-slice_fusion.2), channel_id=1, source_target_pairs={{1,0},{0,1},{3,2},{2,3},{5,4},{4,5},{7,6},{6,7},{9,8},{8,9},{11,10... | collective-permute-start | bytes 6291464 | tf_op jit(solution)/shard_map/ppermute | solution.py:275
  447.7 53.4 %collective-permute-start.11 = (f32[2,32,128,128]{3,2,1,0:T(8,128)}, f32[2,32,128,128]{3,2,1,0:T(8,128)S(1)}, u32[]{:S(2)}, u32[]{:S(2)}) collective-permute-start(f32[2,32,128,128]{3,2,1,0:T(8,128)} %get-tuple-element.31), channel_id=1, source_target_pairs={{1,0},{0,1},{3,2},{2,3},{5,4},{4,5},{7,6},{6,7},{9,8},{8,9},{11,10... | collective-permute-start | bytes 12582920 | tf_op jit(solution)/shard_map/ppermute | solution.py:275
  447.7 53.5 %collective-permute-start.12 = (f32[2,32,128,128]{3,2,1,0:T(8,128)S(1)}, f32[2,32,128,128]{3,2,1,0:T(8,128)}, u32[]{:S(2)}, u32[]{:S(2)}) collective-permute-start(f32[2,32,128,128]{3,2,1,0:T(8,128)S(1)} %get-tuple-element.30), channel_id=1, source_target_pairs={{1,0},{0,1},{3,2},{2,3},{5,4},{4,5},{7,6},{6,7},{9,8},{8,9},{11,10... | collective-permute-start | bytes 12582920 | tf_op jit(solution)/shard_map/ppermute | solution.py:275
  450.8 48.7 %collective-permute-start.16 = (f32[32,128,128]{2,1,0:T(8,128)}, f32[32,128,128]{2,1,0:T(8,128)S(1)}, u32[]{:S(2)}, u32[]{:S(2)}) collective-permute-start(f32[32,128,128]{2,1,0:T(8,128)} %get-tuple-element.36), channel_id=1, source_target_pairs={{2,0},{3,1},{0,2},{1,3},{6,4},{7,5},{4,6},{5,7},{10,8},{11,9},{8,1... | collective-permute-start | bytes 6291464 | tf_op jit(solution)/shard_map/ppermute | solution.py:269
  464.2 80.3 %collective-permute-start.15 = (f32[32,128,128]{2,1,0:T(8,128)}, f32[32,128,128]{2,1,0:T(8,128)S(1)}, u32[]{:S(2)}, u32[]{:S(2)}) collective-permute-start(f32[32,128,128]{2,1,0:T(8,128)} %collective-permute-done.14), channel_id=1, source_target_pairs={{2,0},{3,1},{0,2},{1,3},{6,4},{7,5},{4,6},{5,7},{10,8},{11,9},{8,1... | collective-permute-start | bytes 6291464 | tf_op jit(solution)/shard_map/ppermute | solution.py:269
  499.5 50.4 %collective-permute-start.19 = (f32[32,128,128]{2,1,0:T(8,128)}, f32[32,128,128]{2,1,0:T(8,128)}, u32[]{:S(2)}, u32[]{:S(2)}) collective-permute-start(f32[32,128,128]{2,1,0:T(8,128)} %get-tuple-element.35), channel_id=1, source_target_pairs={{1,0},{0,1},{3,2},{2,3},{5,4},{4,5},{7,6},{6,7},{9,8},{8,9},{11,10... | collective-permute-start | bytes 6291464 | tf_op jit(solution)/shard_map/ppermute | solution.py:275
  499.5 90.0 %collective-permute-start.18 = (f32[32,128,128]{2,1,0:T(8,128)}, f32[32,128,128]{2,1,0:T(8,128)}, u32[]{:S(2)}, u32[]{:S(2)}) collective-permute-start(f32[32,128,128]{2,1,0:T(8,128)} %get-tuple-element.34), channel_id=1, source_target_pairs={{2,0},{3,1},{0,2},{1,3},{6,4},{7,5},{4,6},{5,7},{10,8},{11,9},{8,1... | collective-permute-start | bytes 6291464 | tf_op jit(solution)/shard_map/ppermute | solution.py:269
  501.1 136.6 %collective-permute-start.24 = (f32[32,128,128]{2,1,0:T(8,128)}, f32[32,128,128]{2,1,0:T(8,128)}, u32[]{:S(2)}, u32[]{:S(2)}) collective-permute-start(f32[32,128,128]{2,1,0:T(8,128)} %get-tuple-element.32), channel_id=1, source_target_pairs={{1,0},{0,1},{3,2},{2,3},{5,4},{4,5},{7,6},{6,7},{9,8},{8,9},{11,10... | collective-permute-start | bytes 6291464 | tf_op jit(solution)/shard_map/ppermute | solution.py:275
  501.2 133.2 %collective-permute-start.22 = (f32[32,128,128]{2,1,0:T(8,128)}, f32[32,128,128]{2,1,0:T(8,128)}, u32[]{:S(2)}, u32[]{:S(2)}) collective-permute-start(f32[32,128,128]{2,1,0:T(8,128)} %collective-permute-done.21), channel_id=1, source_target_pairs={{2,0},{3,1},{0,2},{1,3},{6,4},{7,5},{4,6},{5,7},{10,8},{11,9},{8,1... | collective-permute-start | bytes 6291464 | tf_op jit(solution)/shard_map/ppermute | solution.py:269
  545.8 188.0 %collective-permute-start.13 = (f32[2,32,128,128]{3,2,1,0:T(8,128)}, f32[2,32,128,128]{3,2,1,0:T(8,128)}, u32[]{:S(2)}, u32[]{:S(2)}) collective-permute-start(f32[2,32,128,128]{3,2,1,0:T(8,128)} %get-tuple-element.28), channel_id=1, source_target_pairs={{2,0},{3,1},{0,2},{1,3},{6,4},{7,5},{4,6},{5,7},{10,8},{11,9},{8,1... | collective-permute-start | bytes 12582920 | tf_op jit(solution)/shard_map/ppermute | solution.py:269
  549.9 96.3 %collective-permute-start.17 = (f32[32,128,128]{2,1,0:T(8,128)S(1)}, f32[32,128,128]{2,1,0:T(8,128)}, u32[]{:S(2)}, u32[]{:S(2)}) collective-permute-start(f32[32,128,128]{2,1,0:T(8,128)S(1)} %fusion.3), channel_id=1, source_target_pairs={{4,0},{8,4},{12,8},{16,12},{20,16},{24,20},{28,24},{0,28},{5,1},{9... | collective-permute-start | bytes 6291464 | tf_op jit(solution)/shard_map/ppermute | solution.py:280
  589.5 59.6 %collective-permute-start.20 = (f32[32,128,128]{2,1,0:T(8,128)}, f32[32,128,128]{2,1,0:T(8,128)}, u32[]{:S(2)}, u32[]{:S(2)}) collective-permute-start(f32[32,128,128]{2,1,0:T(8,128)} %add.86), channel_id=1, source_target_pairs={{4,0},{8,4},{12,8},{16,12},{20,16},{24,20},{28,24},{0,28},{5,1},{9... | collective-permute-start | bytes 6291464 | tf_op jit(solution)/shard_map/ppermute | solution.py:280
  634.4 54.8 %collective-permute-start.23 = (f32[32,128,128]{2,1,0:T(8,128)}, f32[32,128,128]{2,1,0:T(8,128)}, u32[]{:S(2)}, u32[]{:S(2)}) collective-permute-start(f32[32,128,128]{2,1,0:T(8,128)} %fusion.2), channel_id=1, source_target_pairs={{4,0},{8,4},{12,8},{16,12},{20,16},{24,20},{28,24},{0,28},{5,1},{9... | collective-permute-start | bytes 6291464 | tf_op jit(solution)/shard_map/ppermute | solution.py:280
  641.5 90.5 %collective-permute-start.25 = (f32[32,128,128]{2,1,0:T(8,128)}, f32[32,128,128]{2,1,0:T(8,128)}, u32[]{:S(2)}, u32[]{:S(2)}) collective-permute-start(f32[32,128,128]{2,1,0:T(8,128)} %add.91), channel_id=1, source_target_pairs={{4,0},{8,4},{12,8},{16,12},{20,16},{24,20},{28,24},{0,28},{5,1},{9... | collective-permute-start | bytes 6291464 | tf_op jit(solution)/shard_map/ppermute | solution.py:280
  (12 other events, 101.8 us)
where the time goes:
time: 744 us; the launch traced here: 743 us
  waiting for transfers between devices  478 us (64%)
  Pallas kernels  137 us (18%)
  local copies, waits for them, and re-layouts  59.7 us (8%)
  other arithmetic  39.3 us (5%)
  starting transfers between devices  28.5 us (4%)
    ppermute x6, waiting for transfers between devices, along_band(): lax.ppermute(block, 'band', [((i - distance) % size, i) for i in range(si...  250 us
    ppermute x8, waiting for transfers between devices, from_slow(): lax.ppermute(block, 'grid', [((x + shift) % a * b + c, x * b + c) for x i...  219 us
    pallas_call x2, Pallas kernels, solve(): pl.pallas_call(body, grid_spec=pltpu.PrefetchScalarGridSpec(num_scalar_pr...  137 us
  transfers between devices with their start and end apart: 26, of which 11 were waited for; matrix products, arithmetic and copies ran while one was open for 10% of the time, Pallas kernels for 9%

commit v1 on v0

--- a/solution.py
+++ b/solution.py
@@ -48,7 +48,9 @@
     vis_refs = refs[2:2 + a * b]
     rest = list(refs[2 + a * b:])
     prev_ref = rest.pop(0) if accumulate else None
-    lyf, lyi, rxf, rxi, lzf, lzi, own_out, part_out, re_s, im_s, st_l, st_r, st_z2, ksq, vis_ref = rest
+    lyf, lyi, rxf, rxi, lzf, lzi, own_out = rest[:7]
+    part_outs = rest[7:7 + a * b]
+    re_s, im_s, st_l, st_r, st_z2, ksq, vis_ref = rest[7 + a * b:]
     st_z = st_l
     step = pl.program_id(0)
     na = nz // pz
@@ -192,9 +194,16 @@
                     o = vb * v
                     own_out[0, 1, p] = o + prev_ref[0, 1, p] if accumulate else o
                     pt = pt + vb * own_ref[0, 1, p]
-                part_out[0, p] = pt
+                vis_ref[p] = pt
 
         pipeline(spectrum, xinverse, yinverse, pz, chunk)
+        for dx in range(a):
+            for dc in range(b):
+                here = ((q_ref[0] + dx) % a) * b + (q_ref[1] + dc) % b
+
+                @pl.when(natural == here)
+                def _(dx=dx, dc=dc):
+                    part_outs[dx * b + dc][...] = vis_ref[...]
 
 
 def solve(q, own, vis, prev, pieces, scale, pz=8, py=8, chunk=2, pad=8, zchunk=None, lag=1):
@@ -231,7 +240,12 @@
     ]
     prev_in = pl.BlockSpec((1, n_own, pz, ny, nx), lambda i, q: (zout(i, q)[0], 0, zout(i, q)[1], 0, 0))
     own_o = pl.BlockSpec((1, n_own, pz, ny, nx), lambda i, q: (zout(i, q)[0], 0, zout(i, q)[1], 0, 0))
-    part_o = pl.BlockSpec((1, pz, ny, nx), lambda i, q: (zout(i, q)[0], zout(i, q)[1], 0, 0))
+
+    def part_blk(i, q, dx, dc):
+        here = ((q[0] + dx) % a) * b + (q[1] + dc) % b
+        return (jnp.clip(i - na - nb - here * per, 0, per - 1), 0, 0)
+
+    part_o = [pl.BlockSpec((pz, ny, nx), functools.partial(part_blk, dx=r // b, dc=r % b)) for r in range(a * b)]
     tabs = [left_table(ny, False), left_table(ny, True), right_table(nx, False), right_table(nx, True), left_table(nz, False), left_table(nz, True)]
     tab_specs = [pl.BlockSpec(t.shape, lambda i, q: (0, 0), pipeline_mode=pl.Buffered(1)) for t in tabs]
     pitch = ny + pad
@@ -242,13 +256,13 @@
     return pl.pallas_call(
         body,
         grid_spec=pltpu.PrefetchScalarGridSpec(
-            num_scalar_prefetch=1, grid=(2 * na + nb,), in_specs=specs, out_specs=[own_o, part_o],
+            num_scalar_prefetch=1, grid=(2 * na + nb,), in_specs=specs, out_specs=[own_o] + part_o,
             scratch_shapes=[pltpu.VMEM((nz * pitch, nx), F32), pltpu.VMEM((nz * pitch, nx), F32),
                             pltpu.VMEM((4 * max(ny, nz), max(pz, py) * nx), BF), pltpu.VMEM((pz * ny, 4 * nx), BF),
                             pltpu.VMEM((4 * nz, py * nx), BF), pltpu.VMEM((nz, nx), F32),
                             pltpu.VMEM((pz, ny, nx), F32)]),
-        out_shape=[jax.ShapeDtypeStruct(own.shape, F32), jax.ShapeDtypeStruct((a * b, planes, ny, nx), F32)],
-        compiler_params=pltpu.CompilerParams(vmem_limit_bytes=58 * 2**20),
+        out_shape=[jax.ShapeDtypeStruct(own.shape, F32), *[jax.ShapeDtypeStruct((planes, ny, nx), F32)] * (a * b)],
+        compiler_params=pltpu.CompilerParams(vmem_limit_bytes=60 * 2**20),
         cost_estimate=pl.CostEstimate(flops=flops, bytes_accessed=64 * 2**20, transcendentals=0),
     )(q, *ins)
 
@@ -292,7 +306,7 @@
     q = jnp.stack([x, c]).astype(jnp.int32)
     scale = -FRACTION * 4.0 * math.pi / (nz * ny * nx)
     pz = math.gcd(planes, 16)
-    py = math.gcd(ny, 32)
+    py = math.gcd(ny, max(8, ny // size))
 
     def own_set(bands, s):
         return lax.dynamic_slice_in_dim(bands, s * n_own, n_own, 0)
@@ -319,19 +333,14 @@
                 vis.append(from_fast(lax.dynamic_slice_in_dim(pieces[dx], (c - dc) % b, 1, 0), a, b, dc))
         partner = None
         for n, (g, w) in enumerate(groups):
-            own_part[n], part = solve(q, own_full[:, g:g + w], vis, own_part[n], (a, b), scale, pz=pz, py=py)
-            partner = part if partner is None else partner + part
-        partner = partner.reshape(a, b, planes, ny, nx)
+            own_part[n], *part = solve(q, own_full[:, g:g + w], vis, own_part[n], (a, b), scale, pz=pz, py=py)
+            partner = part if partner is None else [p + r for p, r in zip(partner, part)]
         back = []
         for dc in range(b):
-            here = [from_fast(partner[dx, dc], a, b, (-dc) % b) for dx in range(a)]
+            here = [from_fast(partner[dx * b + dc], a, b, (-dc) % b) for dx in range(a)]
             got = [from_slow(here[dx], a, b, (-dx) % a) for dx in range(1, a)]
             if last is not None:
-                got, last = lax.optimization_barrier((got, last))
-                if dc:
-                    back[-1] = last
-                else:
-                    returned[-1][-1] = last
+                got, _ = lax.optimization_barrier((got, last))
             last = here[0]
             for piece in got:
                 last = last + piece

time: 744 us -> 743 us (level)
  local copies, waits for them, and re-layouts: 59.7 us -> 51.6 us
    ppermute x8, waiting for transfers between devices: 219 us -> 237 us  [from_slow(): lax.ppermute(block, 'grid', [((x + shift) % a * b + c, x * b + c) for x i...]
    ppermute x12, waiting for transfers between devices: 8.6 us -> 0.03 us  [from_fast(): lax.ppermute(block, 'grid', [(x * b + (c + shift) % b, x * b + c) for x i...]
  transfers between devices with their start and end apart: 26 -> 26, of which waited for: 11 -> 10; matrix products, arithmetic and copies ran while one was open for 10% -> 9% of each run, Pallas kernels for 9% -> 9%
where the time goes in v1:
time: 743 us; the launch traced here: 742 us
  waiting for transfers between devices  482 us (65%)
  Pallas kernels  141 us (19%)
  local copies, waits for them, and re-layouts  51.6 us (7%)
  other arithmetic  38.6 us (5%)
  starting transfers between devices  27.2 us (4%)
    ppermute x6, waiting for transfers between devices, along_band(): lax.ppermute(block, 'band', [((i - distance) % size, i) for i in range(si...  245 us
    ppermute x8, waiting for transfers between devices, from_slow(): lax.ppermute(block, 'grid', [((x + shift) % a * b + c, x * b + c) for x i...  237 us
    pallas_call x2, Pallas kernels, solve(): pl.pallas_call(body, grid_spec=pltpu.PrefetchScalarGridSpec(num_scalar_pr...  141 us
  transfers between devices with their start and end apart: 26, of which 10 were waited for; matrix products, arithmetic and copies ran while one was open for 9% of the time, Pallas kernels for 9%

profile of v1, /device:TPU:0, one launch (start us, length us, event | category | flops | bytes accessed | tf_op | source)
XLA Modules:
  0.0 742.1 jit_solution(3670553586610221)
XLA Ops:
  0.6 4.7 slice.19
  8.3 5.0 constant_dynamic-slice_fusion.5
  19.8 83.3 %collective-permute-done.7.refs_2_ = f32[2,32,128,128]{3,2,1,0:T(8,128)} collective-permute-done((f32[2,32,128,128]{3,2,1,0:T(8,128)}, f32[2,32,128,128]{3,2,1,0:T(8,128)}, u32[]{:S(2)}, u32[]{:S(2)}) %collective-permute-start.7) | collective-permute-done | bytes 4194336 | tf_op jit(solution)/shard_map/ppermute | solution.py:294
  104.8 87.4 %collective-permute-done.3.refs_2_ = f32[2,32,128,128]{3,2,1,0:T(8,128)} collective-permute-done((f32[2,32,128,128]{3,2,1,0:T(8,128)}, f32[2,32,128,128]{3,2,1,0:T(8,128)}, u32[]{:S(2)}, u32[]{:S(2)}) %collective-permute-start.3) | collective-permute-done | bytes 4194336 | tf_op jit(solution)/shard_map/ppermute | solution.py:294
  193.6 4.7 constant_dynamic-slice_fusion.4
  208.7 81.4 %collective-permute-done.5.refs_4_ = f32[2,32,128,128]{3,2,1,0:T(8,128)} collective-permute-done((f32[2,32,128,128]{3,2,1,0:T(8,128)}, f32[2,32,128,128]{3,2,1,0:T(8,128)}, u32[]{:S(2)}, u32[]{:S(2)}) %collective-permute-start.5) | collective-permute-done | bytes 4194336 | tf_op jit(solution)/shard_map/ppermute | solution.py:283
  293.8 10.8 %pad_maximum_fusion.refs_1_ = f32[4,2,32,128,128]{4,3,2,1,0:T(8,128)} fusion(f32[1,2,32,128,128]{4,3,2,1,0:T(8,128)} %bitcast.5, f32[1,2,32,128,128]{4,3,2,1,0:T(8,128)} %bitcast.4, f32[1,2,32,128,128]{4,3,2,1,0:T(8,128)} %bitcast.3, f32[1,2,32,128,128]{4,3,2,1,0:T(8,128)S(1)} %fusion.2), kind=kLoop, calls=%fused_computation | loop fusion | flops 12582912 | bytes 33554432 | tf_op jit(solution)/shard_map/stack | solution.py:321
  305.9 69.6 %shard_map.149 = (f32[4,2,32,128,128]{4,3,2,1,0:T(8,128)}, f32[32,128,128]{2,1,0:T(8,128)}, f32[32,128,128]{2,1,0:T(8,128)}, f32[32,128,128]{2,1,0:T(8,128)}, f32[32,128,128]{2,1,0:T(8,128)}) custom-call(s32[2]{0:T(128)} %pad_add_fusion.refs_0_, f32[4,2,32,128,128]{4,3,2,1,0:T(8,128)} %pad_maximum_fusion.refs_1_, ...), custom_call_target="tpu_custom_call" | custom-call | flops 38654705664 | bytes 67108864 | tf_op jit(solution)/shard_map/pallas_call | solution.py:256
  375.5 71.8 %shard_map.150 = (f32[4,2,32,128,128]{4,3,2,1,0:T(8,128)}, f32[32,128,128]{2,1,0:T(8,128)}, f32[32,128,128]{2,1,0:T(8,128)}, f32[32,128,128]{2,1,0:T(8,128)}, f32[32,128,128]{2,1,0:T(8,128)}) custom-call(s32[2]{0:T(128)} %pad_add_fusion.refs_0_, f32[4,2,32,128,128]{4,3,2,1,0:T(8,128)} %pad_maximum_fusion.refs_1_, ...), custom_call_target="tpu_custom_call" | custom-call | flops 38654705664 | bytes 67108864 | tf_op jit(solution)/shard_map/pallas_call | solution.py:256
  447.3 4.2 slice_bitcast_fusion
  454.0 45.7 %collective-permute-done.14 = f32[32,128,128]{2,1,0:T(8,128)S(1)} collective-permute-done((f32[32,128,128]{2,1,0:T(8,128)S(1)}, f32[32,128,128]{2,1,0:T(8,128)S(1)}, u32[]{:S(2)}, u32[]{:S(2)}) %collective-permute-start.14) | collective-permute-done | bytes 2097184 | tf_op jit(solution)/shard_map/ppermute | solution.py:283
  503.3 10.3 %fusion = (f32[2,32,128,128]{3,2,1,0:T(8,128)}, f32[2,32,128,128]{3,2,1,0:T(8,128)}) fusion(f32[2,32,128,128]{3,2,1,0:T(8,128)} %collective-permute-done.12, f32[2,2,2,32,128,128]{5,4,3,2,1,0:T(8,128)} %bitcast.29, f32[2,32,128,128]{3,2,1,0:T(8,128)S(1)} %collective-permute-done.11), kind=kLoop, calls=%fused_computation.4 | loop fusion | flops 2097152 | bytes 25165824 | tf_op jit(solution)/shard_map/add | solution.py:355
  514.3 3.3 add.83
  517.5 31.1 %collective-permute-done.18 = f32[32,128,128]{2,1,0:T(8,128)} collective-permute-done((f32[32,128,128]{2,1,0:T(8,128)}, f32[32,128,128]{2,1,0:T(8,128)}, u32[]{:S(2)}, u32[]{:S(2)}) %collective-permute-start.18) | collective-permute-done | bytes 2097184 | tf_op jit(solution)/shard_map/ppermute | solution.py:283
  554.3 39.3 %collective-permute-done.20 = f32[32,128,128]{2,1,0:T(8,128)} collective-permute-done((f32[32,128,128]{2,1,0:T(8,128)}, f32[32,128,128]{2,1,0:T(8,128)}, u32[]{:S(2)}, u32[]{:S(2)}) %collective-permute-start.20) | collective-permute-done | bytes 2097184 | tf_op jit(solution)/shard_map/ppermute | solution.py:283
  596.8 3.3 add.88
  600.0 38.5 %collective-permute-done.24 = f32[32,128,128]{2,1,0:T(8,128)} collective-permute-done((f32[32,128,128]{2,1,0:T(8,128)}, f32[32,128,128]{2,1,0:T(8,128)}, u32[]{:S(2)}, u32[]{:S(2)}) %collective-permute-start.24) | collective-permute-done | bytes 2097184 | tf_op jit(solution)/shard_map/ppermute | solution.py:283
  638.5 3.2 collective-permute-start.21
  641.7 3.9 add.91
  646.2 4.0 pad_maximum_fusion.1
  654.9 33.1 %collective-permute-done.21 = f32[32,128,128]{2,1,0:T(8,128)} collective-permute-done((f32[32,128,128]{2,1,0:T(8,128)}, f32[32,128,128]{2,1,0:T(8,128)}, u32[]{:S(2)}, u32[]{:S(2)}) %collective-permute-start.21) | collective-permute-done | bytes 2097184 | tf_op jit(solution)/shard_map/ppermute | solution.py:294
  689.8 41.2 %collective-permute-done.25 = f32[32,128,128]{2,1,0:T(8,128)} collective-permute-done((f32[32,128,128]{2,1,0:T(8,128)}, f32[32,128,128]{2,1,0:T(8,128)}, u32[]{:S(2)}, u32[]{:S(2)}) %collective-permute-start.25) | collective-permute-done | bytes 2097184 | tf_op jit(solution)/shard_map/ppermute | solution.py:294
  732.9 5.8 constant_dynamic-update-slice_fusion
  738.7 3.4 copy-done
  (74 shorter events, 52.3 us)
Async XLA Ops:
  5.3 97.8 %collective-permute-start.7 = (f32[2,32,128,128]{3,2,1,0:T(8,128)}, f32[2,32,128,128]{3,2,1,0:T(8,128)}, u32[]{:S(2)}, u32[]{:S(2)}) collective-permute-start(f32[2,32,128,128]{3,2,1,0:T(8,128)} %slice.19), channel_id=1, source_target_pairs={{28,0},{0,4},{4,8},{8,12},{12,16},{16,20},{20,24},{24,28},{29,1},{... | collective-permute-start | bytes 12582920 | tf_op jit(solution)/shard_map/ppermute | solution.py:294
  16.8 175.4 %collective-permute-start.3 = (f32[2,32,128,128]{3,2,1,0:T(8,128)}, f32[2,32,128,128]{3,2,1,0:T(8,128)}, u32[]{:S(2)}, u32[]{:S(2)}) collective-permute-start(f32[2,32,128,128]{3,2,1,0:T(8,128)} %slice.18), channel_id=1, source_target_pairs={{28,0},{0,4},{4,8},{8,12},{12,16},{16,20},{20,24},{24,28},{29,1},{... | collective-permute-start | bytes 12582920 | tf_op jit(solution)/shard_map/ppermute | solution.py:294
  18.3 180.0 %collective-permute-start.1 = (f32[2,32,128,128]{3,2,1,0:T(8,128)}, f32[2,32,128,128]{3,2,1,0:T(8,128)}, u32[]{:S(2)}, u32[]{:S(2)}) collective-permute-start(f32[2,32,128,128]{3,2,1,0:T(8,128)} %constant_dynamic-slice_fusion.5), channel_id=1, source_target_pairs={{2,0},{3,1},{0,2},{1,3},{6,4},{7,5},{4,6},{5,7},{10,8},{11,9},{8,1... | collective-permute-start | bytes 12582920 | tf_op jit(solution)/shard_map/ppermute | solution.py:283
  103.1 98.8 %collective-permute-start.9 = (f32[2,32,128,128]{3,2,1,0:T(8,128)}, f32[2,32,128,128]{3,2,1,0:T(8,128)}, u32[]{:S(2)}, u32[]{:S(2)}) collective-permute-start(f32[2,32,128,128]{3,2,1,0:T(8,128)} %collective-permute-done.7.refs_2_), channel_id=1, source_target_pairs={{2,0},{3,1},{0,2},{1,3},{6,4},{7,5},{4,6},{5,7},{10,8},{11,9},{8,1... | collective-permute-start | bytes 12582920 | tf_op jit(solution)/shard_map/ppermute | solution.py:283
  192.1 98.0 %collective-permute-start.5 = (f32[2,32,128,128]{3,2,1,0:T(8,128)}, f32[2,32,128,128]{3,2,1,0:T(8,128)}, u32[]{:S(2)}, u32[]{:S(2)}) collective-permute-start(f32[2,32,128,128]{3,2,1,0:T(8,128)} %collective-permute-done.3.refs_2_), channel_id=1, source_target_pairs={{2,0},{3,1},{0,2},{1,3},{6,4},{7,5},{4,6},{5,7},{10,8},{11,9},{8,1... | collective-permute-start | bytes 12582920 | tf_op jit(solution)/shard_map/ppermute | solution.py:283
  198.3 94.9 %collective-permute-start = (f32[2,32,128,128]{3,2,1,0:T(8,128)}, f32[2,32,128,128]{3,2,1,0:T(8,128)}, u32[]{:S(2)}, u32[]{:S(2)}) collective-permute-start(f32[2,32,128,128]{3,2,1,0:T(8,128)} %constant_dynamic-slice_fusion.4), channel_id=1, source_target_pairs={{1,0},{0,1},{3,2},{2,3},{5,4},{4,5},{7,6},{6,7},{9,8},{8,9},{11,10... | collective-permute-start | bytes 12582920 | tf_op jit(solution)/shard_map/ppermute | solution.py:289
  198.3 95.4 %collective-permute-start.2 = (f32[2,32,128,128]{3,2,1,0:T(8,128)}, f32[2,32,128,128]{3,2,1,0:T(8,128)}, u32[]{:S(2)}, u32[]{:S(2)}) collective-permute-start(f32[2,32,128,128]{3,2,1,0:T(8,128)} %collective-permute-done.1), channel_id=1, source_target_pairs={{1,0},{0,1},{3,2},{2,3},{5,4},{4,5},{7,6},{6,7},{9,8},{8,9},{11,10... | collective-permute-start | bytes 12582920 | tf_op jit(solution)/shard_map/ppermute | solution.py:289
  200.6 104.0 %collective-permute-start.8 = (f32[1,32,128,128]{3,2,1,0:T(8,128)S(1)}, f32[1,32,128,128]{3,2,1,0:T(8,128)S(1)}, u32[]{:S(2)}, u32[]{:S(2)}) collective-permute-start(f32[1,32,128,128]{3,2,1,0:T(8,128)S(1)} %constant_dynamic-slice_fusion.1), channel_id=1, source_target_pairs={{1,0},{0,1},{3,2},{2,3},{5,4},{4,5},{7,6},{6,7},{9,8},{8,9},{11,10... | collective-permute-start | bytes 6291464 | tf_op jit(solution)/shard_map/ppermute | solution.py:289
  203.7 102.2 %collective-permute-start.10 = (f32[1,32,128,128]{3,2,1,0:T(8,128)S(1)}, f32[1,32,128,128]{3,2,1,0:T(8,128)}, u32[]{:S(2)}, u32[]{:S(2)}) collective-permute-start(f32[1,32,128,128]{3,2,1,0:T(8,128)S(1)} %constant_dynamic-slice_fusion), channel_id=1, source_target_pairs={{1,0},{0,1},{3,2},{2,3},{5,4},{4,5},{7,6},{6,7},{9,8},{8,9},{11,10... | collective-permute-start | bytes 6291464 | tf_op jit(solution)/shard_map/ppermute | solution.py:289
  290.1 85.3 %collective-permute-start.4 = (f32[1,32,128,128]{3,2,1,0:T(8,128)S(1)}, f32[1,32,128,128]{3,2,1,0:T(8,128)}, u32[]{:S(2)}, u32[]{:S(2)}) collective-permute-start(f32[1,32,128,128]{3,2,1,0:T(8,128)S(1)} %constant_dynamic-slice_fusion.3), channel_id=1, source_target_pairs={{1,0},{0,1},{3,2},{2,3},{5,4},{4,5},{7,6},{6,7},{9,8},{8,9},{11,10... | collective-permute-start | bytes 6291464 | tf_op jit(solution)/shard_map/ppermute | solution.py:289
  293.3 82.2 %collective-permute-start.6 = (f32[1,32,128,128]{3,2,1,0:T(8,128)}, f32[1,32,128,128]{3,2,1,0:T(8,128)}, u32[]{:S(2)}, u32[]{:S(2)}) collective-permute-start(f32[1,32,128,128]{3,2,1,0:T(8,128)} %constant_dynamic-slice_fusion.2), channel_id=1, source_target_pairs={{1,0},{0,1},{3,2},{2,3},{5,4},{4,5},{7,6},{6,7},{9,8},{8,9},{11,10... | collective-permute-start | bytes 6291464 | tf_op jit(solution)/shard_map/ppermute | solution.py:289
  451.5 50.3 %collective-permute-start.11 = (f32[2,32,128,128]{3,2,1,0:T(8,128)S(1)}, f32[2,32,128,128]{3,2,1,0:T(8,128)S(1)}, u32[]{:S(2)}, u32[]{:S(2)}) collective-permute-start(f32[2,32,128,128]{3,2,1,0:T(8,128)S(1)} %get-tuple-element.37), channel_id=1, source_target_pairs={{1,0},{0,1},{3,2},{2,3},{5,4},{4,5},{7,6},{6,7},{9,8},{8,9},{11,10... | collective-permute-start | bytes 12582920 | tf_op jit(solution)/shard_map/ppermute | solution.py:289
  451.6 50.2 %collective-permute-start.12 = (f32[2,32,128,128]{3,2,1,0:T(8,128)S(1)}, f32[2,32,128,128]{3,2,1,0:T(8,128)}, u32[]{:S(2)}, u32[]{:S(2)}) collective-permute-start(f32[2,32,128,128]{3,2,1,0:T(8,128)S(1)} %get-tuple-element.36), channel_id=1, source_target_pairs={{1,0},{0,1},{3,2},{2,3},{5,4},{4,5},{7,6},{6,7},{9,8},{8,9},{11,10... | collective-permute-start | bytes 12582920 | tf_op jit(solution)/shard_map/ppermute | solution.py:289
  452.1 47.6 %collective-permute-start.14 = (f32[32,128,128]{2,1,0:T(8,128)S(1)}, f32[32,128,128]{2,1,0:T(8,128)S(1)}, u32[]{:S(2)}, u32[]{:S(2)}) collective-permute-start(f32[32,128,128]{2,1,0:T(8,128)S(1)} %copy-done.7), channel_id=1, source_target_pairs={{2,0},{3,1},{0,2},{1,3},{6,4},{7,5},{4,6},{5,7},{10,8},{11,9},{8,1... | collective-permute-start | bytes 6291464 | tf_op jit(solution)/shard_map/ppermute | solution.py:283
  453.5 47.7 %collective-permute-start.23 = (f32[32,128,128]{2,1,0:T(8,128)S(1)}, f32[32,128,128]{2,1,0:T(8,128)}, u32[]{:S(2)}, u32[]{:S(2)}) collective-permute-start(f32[32,128,128]{2,1,0:T(8,128)S(1)} %copy-done.8), channel_id=1, source_target_pairs={{1,0},{0,1},{3,2},{2,3},{5,4},{4,5},{7,6},{6,7},{9,8},{8,9},{11,10... | collective-permute-start | bytes 6291464 | tf_op jit(solution)/shard_map/ppermute | solution.py:289
  499.7 48.9 %collective-permute-start.18 = (f32[32,128,128]{2,1,0:T(8,128)}, f32[32,128,128]{2,1,0:T(8,128)}, u32[]{:S(2)}, u32[]{:S(2)}) collective-permute-start(f32[32,128,128]{2,1,0:T(8,128)} %collective-permute-done.17), channel_id=1, source_target_pairs={{2,0},{3,1},{0,2},{1,3},{6,4},{7,5},{4,6},{5,7},{10,8},{11,9},{8,1... | collective-permute-start | bytes 6291464 | tf_op jit(solution)/shard_map/ppermute | solution.py:283
  501.2 92.3 %collective-permute-start.20 = (f32[32,128,128]{2,1,0:T(8,128)}, f32[32,128,128]{2,1,0:T(8,128)}, u32[]{:S(2)}, u32[]{:S(2)}) collective-permute-start(f32[32,128,128]{2,1,0:T(8,128)} %get-tuple-element.29), channel_id=1, source_target_pairs={{2,0},{3,1},{0,2},{1,3},{6,4},{7,5},{4,6},{5,7},{10,8},{11,9},{8,1... | collective-permute-start | bytes 6291464 | tf_op jit(solution)/shard_map/ppermute | solution.py:283
  501.8 139.9 %collective-permute-start.22 = (f32[32,128,128]{2,1,0:T(8,128)}, f32[32,128,128]{2,1,0:T(8,128)}, u32[]{:S(2)}, u32[]{:S(2)}) collective-permute-start(f32[32,128,128]{2,1,0:T(8,128)} %get-tuple-element.31), channel_id=1, source_target_pairs={{1,0},{0,1},{3,2},{2,3},{5,4},{4,5},{7,6},{6,7},{9,8},{8,9},{11,10... | collective-permute-start | bytes 6291464 | tf_op jit(solution)/shard_map/ppermute | solution.py:289
  501.9 136.6 %collective-permute-start.24 = (f32[32,128,128]{2,1,0:T(8,128)}, f32[32,128,128]{2,1,0:T(8,128)}, u32[]{:S(2)}, u32[]{:S(2)}) collective-permute-start(f32[32,128,128]{2,1,0:T(8,128)} %collective-permute-done.23), channel_id=1, source_target_pairs={{2,0},{3,1},{0,2},{1,3},{6,4},{7,5},{4,6},{5,7},{10,8},{11,9},{8,1... | collective-permute-start | bytes 6291464 | tf_op jit(solution)/shard_map/ppermute | solution.py:283
  513.6 219.2 %collective-permute-start.13 = (f32[2,32,128,128]{3,2,1,0:T(8,128)}, f32[2,32,128,128]{3,2,1,0:T(8,128)}, u32[]{:S(2)}, u32[]{:S(2)}) collective-permute-start(f32[2,32,128,128]{3,2,1,0:T(8,128)} %get-tuple-element.34), channel_id=1, source_target_pairs={{2,0},{3,1},{0,2},{1,3},{6,4},{7,5},{4,6},{5,7},{10,8},{11,9},{8,1... | collective-permute-start | bytes 12582920 | tf_op jit(solution)/shard_map/ppermute | solution.py:283
  548.6 101.6 %collective-permute-start.15 = (f32[32,128,128]{2,1,0:T(8,128)}, f32[32,128,128]{2,1,0:T(8,128)}, u32[]{:S(2)}, u32[]{:S(2)}) collective-permute-start(f32[32,128,128]{2,1,0:T(8,128)} %add.83), channel_id=1, source_target_pairs={{4,0},{8,4},{12,8},{16,12},{20,16},{24,20},{28,24},{0,28},{5,1},{9... | collective-permute-start | bytes 6291464 | tf_op jit(solution)/shard_map/ppermute | solution.py:294
  593.6 59.5 %collective-permute-start.19 = (f32[32,128,128]{2,1,0:T(8,128)S(1)}, f32[32,128,128]{2,1,0:T(8,128)}, u32[]{:S(2)}, u32[]{:S(2)}) collective-permute-start(f32[32,128,128]{2,1,0:T(8,128)S(1)} %add.86), channel_id=1, source_target_pairs={{4,0},{8,4},{12,8},{16,12},{20,16},{24,20},{28,24},{0,28},{5,1},{9... | collective-permute-start | bytes 6291464 | tf_op jit(solution)/shard_map/ppermute | solution.py:294
  638.5 49.5 %collective-permute-start.21 = (f32[32,128,128]{2,1,0:T(8,128)}, f32[32,128,128]{2,1,0:T(8,128)}, u32[]{:S(2)}, u32[]{:S(2)}) collective-permute-start(f32[32,128,128]{2,1,0:T(8,128)} %add.88), channel_id=1, source_target_pairs={{4,0},{8,4},{12,8},{16,12},{20,16},{24,20},{28,24},{0,28},{5,1},{9... | collective-permute-start | bytes 6291464 | tf_op jit(solution)/shard_map/ppermute | solution.py:294
  645.6 85.5 %collective-permute-start.25 = (f32[32,128,128]{2,1,0:T(8,128)}, f32[32,128,128]{2,1,0:T(8,128)}, u32[]{:S(2)}, u32[]{:S(2)}) collective-permute-start(f32[32,128,128]{2,1,0:T(8,128)} %add.91), channel_id=1, source_target_pairs={{4,0},{8,4},{12,8},{16,12},{20,16},{24,20},{28,24},{0,28},{5,1},{9... | collective-permute-start | bytes 6291464 | tf_op jit(solution)/shard_map/ppermute | solution.py:294
  (12 other events, 187.8 us)

commit v2 on v1

--- a/solution.py
+++ b/solution.py
@@ -356,8 +356,9 @@
         if dx == 0:
             own_out = jnp.concatenate([summed] * a, axis=0)
             continue
-        got = from_slow(summed, a, b, (-dx) % a)
-        own_out = lax.dynamic_update_slice_in_dim(own_out, got, ((x - dx) % a) * n_own, 0)
+        for i in range(n_own):
+            got = from_slow(summed[i:i + 1], a, b, (-dx) % a)
+            own_out = lax.dynamic_update_slice_in_dim(own_out, got, ((x - dx) % a) * n_own + i, 0)
     partner_out = jnp.zeros_like(travel_bands)
     for k in range(n_vis):
         for dc in range(b):

time: 743 us -> 710 us (0.956)
  waiting for transfers between devices: 482 us -> 448 us
    ppermute x6, waiting for transfers between devices: 245 us -> 212 us  [along_band(): lax.ppermute(block, 'band', [((i - distance) % size, i) for i in range(si...]
    ppermute x8 -> x9, waiting for transfers between devices: 237 us -> 215 us  [from_slow(): lax.ppermute(block, 'grid', [((x + shift) % a * b + c, x * b + c) for x i...]
    ppermute x12, waiting for transfers between devices: 0.03 us -> 20.3 us  [from_fast(): lax.ppermute(block, 'grid', [(x * b + (c + shift) % b, x * b + c) for x i...]
  transfers between devices with their start and end apart: 26 -> 27, of which waited for: 10 -> 13; matrix products, arithmetic and copies ran while one was open for 9% -> 11% of each run, Pallas kernels for 9% -> 20%
where the time goes in v2:
time: 710 us; the launch traced here: 709 us
  waiting for transfers between devices  448 us (63%)
  Pallas kernels  142 us (20%)
  local copies, waits for them, and re-layouts  56.8 us (8%)
  other arithmetic  36.3 us (5%)
  starting transfers between devices  25.4 us (4%)
    ppermute x9, waiting for transfers between devices, from_slow(): lax.ppermute(block, 'grid', [((x + shift) % a * b + c, x * b + c) for x i...  215 us
    ppermute x6, waiting for transfers between devices, along_band(): lax.ppermute(block, 'band', [((i - distance) % size, i) for i in range(si...  212 us
    pallas_call x2, Pallas kernels, solve(): pl.pallas_call(body, grid_spec=pltpu.PrefetchScalarGridSpec(num_scalar_pr...  142 us
    ppermute x12, waiting for transfers between devices, from_fast(): lax.ppermute(block, 'grid', [(x * b + (c + shift) % b, x * b + c) for x i...  20.3 us
    ppermute x6, starting transfers between devices, along_band(): lax.ppermute(block, 'band', [((i - distance) % size, i) for i in range(si...  14.7 us
  transfers between devices with their start and end apart: 27, of which 13 were waited for; matrix products, arithmetic and copies ran while one was open for 11% of the time, Pallas kernels for 20%

profile of v2, /device:TPU:0, one launch (start us, length us, event | category | flops | bytes accessed | tf_op | source)
XLA Modules:
  0.0 709.0 jit_solution(6457884207850106092)
XLA Ops:
  0.6 4.7 slice.25
  8.3 5.0 constant_dynamic-slice_fusion.5
  19.8 83.3 %collective-permute-done.7.refs_2_ = f32[2,32,128,128]{3,2,1,0:T(8,128)} collective-permute-done((f32[2,32,128,128]{3,2,1,0:T(8,128)}, f32[2,32,128,128]{3,2,1,0:T(8,128)}, u32[]{:S(2)}, u32[]{:S(2)}) %collective-permute-start.7) | collective-permute-done | bytes 4194336 | tf_op jit(solution)/shard_map/ppermute | solution.py:294
  104.8 87.4 %collective-permute-done.3.refs_2_ = f32[2,32,128,128]{3,2,1,0:T(8,128)} collective-permute-done((f32[2,32,128,128]{3,2,1,0:T(8,128)}, f32[2,32,128,128]{3,2,1,0:T(8,128)}, u32[]{:S(2)}, u32[]{:S(2)}) %collective-permute-start.3) | collective-permute-done | bytes 4194336 | tf_op jit(solution)/shard_map/ppermute | solution.py:294
  193.6 4.7 constant_dynamic-slice_fusion.4
  210.0 80.1 %collective-permute-done.5.refs_4_ = f32[2,32,128,128]{3,2,1,0:T(8,128)} collective-permute-done((f32[2,32,128,128]{3,2,1,0:T(8,128)}, f32[2,32,128,128]{3,2,1,0:T(8,128)}, u32[]{:S(2)}, u32[]{:S(2)}) %collective-permute-start.5) | collective-permute-done | bytes 4194336 | tf_op jit(solution)/shard_map/ppermute | solution.py:283
  293.8 10.8 %pad_maximum_fusion.refs_1_ = f32[4,2,32,128,128]{4,3,2,1,0:T(8,128)} fusion(f32[1,2,32,128,128]{4,3,2,1,0:T(8,128)} %bitcast.5, f32[1,2,32,128,128]{4,3,2,1,0:T(8,128)} %bitcast.4, f32[1,2,32,128,128]{4,3,2,1,0:T(8,128)} %bitcast.3, f32[1,2,32,128,128]{4,3,2,1,0:T(8,128)S(1)} %fusion.3), kind=kLoop, calls=%fused_computation | loop fusion | flops 12582912 | bytes 33554432 | tf_op jit(solution)/shard_map/stack | solution.py:321
  305.9 69.7 %shard_map.149 = (f32[4,2,32,128,128]{4,3,2,1,0:T(8,128)}, f32[32,128,128]{2,1,0:T(8,128)}, f32[32,128,128]{2,1,0:T(8,128)}, f32[32,128,128]{2,1,0:T(8,128)}, f32[32,128,128]{2,1,0:T(8,128)}) custom-call(s32[2]{0:T(128)} %pad_add_fusion.refs_0_, f32[4,2,32,128,128]{4,3,2,1,0:T(8,128)} %pad_maximum_fusion.refs_1_, ...), custom_call_target="tpu_custom_call" | custom-call | flops 38654705664 | bytes 67108864 | tf_op jit(solution)/shard_map/pallas_call | solution.py:256
  377.1 71.9 %shard_map.150 = (f32[4,2,32,128,128]{4,3,2,1,0:T(8,128)}, f32[32,128,128]{2,1,0:T(8,128)}, f32[32,128,128]{2,1,0:T(8,128)}, f32[32,128,128]{2,1,0:T(8,128)}, f32[32,128,128]{2,1,0:T(8,128)}) custom-call(s32[2]{0:T(128)} %pad_add_fusion.refs_0_, f32[4,2,32,128,128]{4,3,2,1,0:T(8,128)} %pad_maximum_fusion.refs_1_, ...), custom_call_target="tpu_custom_call" | custom-call | flops 38654705664 | bytes 67108864 | tf_op jit(solution)/shard_map/pallas_call | solution.py:256
  449.0 4.2 slice_bitcast_fusion
  454.4 15.2 %collective-permute-done.18 = f32[32,128,128]{2,1,0:T(8,128)} collective-permute-done((f32[32,128,128]{2,1,0:T(8,128)S(1)}, f32[32,128,128]{2,1,0:T(8,128)}, u32[]{:S(2)}, u32[]{:S(2)}) %collective-permute-start.18) | collective-permute-done | bytes 2097184 | tf_op jit(solution)/shard_map/ppermute | solution.py:289
  479.8 3.2 collective-permute-start.16
  483.0 10.1 %fusion = (f32[2,32,128,128]{3,2,1,0:T(8,128)S(1)}, f32[2,32,128,128]{3,2,1,0:T(8,128)}) fusion(f32[2,32,128,128]{3,2,1,0:T(8,128)} %copy-done.3, f32[2,2,2,32,128,128]{5,4,3,2,1,0:T(8,128)} %bitcast.29, f32[2,32,128,128]{3,2,1,0:T(8,128)} %collective-permute-done.11), kind=kLoop, calls=%fused_computation.4 | loop fusion | flops 2097152 | bytes 25165824 | tf_op jit(solution)/shard_map/add | solution.py:355
  495.4 23.0 %collective-permute-done.19 = f32[32,128,128]{2,1,0:T(8,128)} collective-permute-done((f32[32,128,128]{2,1,0:T(8,128)}, f32[32,128,128]{2,1,0:T(8,128)}, u32[]{:S(2)}, u32[]{:S(2)}) %collective-permute-start.19) | collective-permute-done | bytes 2097184 | tf_op jit(solution)/shard_map/ppermute | solution.py:283
  520.7 42.7 %collective-permute-done.21 = f32[32,128,128]{2,1,0:T(8,128)} collective-permute-done((f32[32,128,128]{2,1,0:T(8,128)}, f32[32,128,128]{2,1,0:T(8,128)}, u32[]{:S(2)}, u32[]{:S(2)}) %collective-permute-start.21) | collective-permute-done | bytes 2097184 | tf_op jit(solution)/shard_map/ppermute | solution.py:283
  563.4 3.2 collective-permute-start.20
  566.6 3.2 add.99
  569.8 38.5 %collective-permute-done.25 = f32[32,128,128]{2,1,0:T(8,128)} collective-permute-done((f32[32,128,128]{2,1,0:T(8,128)}, f32[32,128,128]{2,1,0:T(8,128)}, u32[]{:S(2)}, u32[]{:S(2)}) %collective-permute-start.25) | collective-permute-done | bytes 2097184 | tf_op jit(solution)/shard_map/ppermute | solution.py:283
  611.5 3.9 add.102
  616.5 4.0 pad_maximum_fusion.1
  623.4 29.9 %collective-permute-done.13 = f32[1,32,128,128]{3,2,1,0:T(8,128)} collective-permute-done((f32[1,32,128,128]{3,2,1,0:T(8,128)}, f32[1,32,128,128]{3,2,1,0:T(8,128)}, u32[]{:S(2)}, u32[]{:S(2)}) %collective-permute-start.13) | collective-permute-done | bytes 2097184 | tf_op jit(solution)/shard_map/ppermute | solution.py:283
  659.6 40.6 %collective-permute-done.26 = f32[32,128,128]{2,1,0:T(8,128)} collective-permute-done((f32[32,128,128]{2,1,0:T(8,128)}, f32[32,128,128]{2,1,0:T(8,128)}, u32[]{:S(2)}, u32[]{:S(2)}) %collective-permute-start.26) | collective-permute-done | bytes 2097184 | tf_op jit(solution)/shard_map/ppermute | solution.py:294
  702.1 3.4 constant_dynamic-update-slice_fusion
  705.6 3.4 copy-done
  (80 shorter events, 62.1 us)
Async XLA Ops:
  5.4 97.8 %collective-permute-start.7 = (f32[2,32,128,128]{3,2,1,0:T(8,128)}, f32[2,32,128,128]{3,2,1,0:T(8,128)}, u32[]{:S(2)}, u32[]{:S(2)}) collective-permute-start(f32[2,32,128,128]{3,2,1,0:T(8,128)} %slice.25), channel_id=1, source_target_pairs={{28,0},{0,4},{4,8},{8,12},{12,16},{16,20},{20,24},{24,28},{29,1},{... | collective-permute-start | bytes 12582920 | tf_op jit(solution)/shard_map/ppermute | solution.py:294
  16.8 175.4 %collective-permute-start.3 = (f32[2,32,128,128]{3,2,1,0:T(8,128)}, f32[2,32,128,128]{3,2,1,0:T(8,128)}, u32[]{:S(2)}, u32[]{:S(2)}) collective-permute-start(f32[2,32,128,128]{3,2,1,0:T(8,128)} %slice.24), channel_id=1, source_target_pairs={{28,0},{0,4},{4,8},{8,12},{12,16},{16,20},{20,24},{24,28},{29,1},{... | collective-permute-start | bytes 12582920 | tf_op jit(solution)/shard_map/ppermute | solution.py:294
  18.3 180.0 %collective-permute-start.1 = (f32[2,32,128,128]{3,2,1,0:T(8,128)}, f32[2,32,128,128]{3,2,1,0:T(8,128)}, u32[]{:S(2)}, u32[]{:S(2)}) collective-permute-start(f32[2,32,128,128]{3,2,1,0:T(8,128)} %constant_dynamic-slice_fusion.5), channel_id=1, source_target_pairs={{2,0},{3,1},{0,2},{1,3},{6,4},{7,5},{4,6},{5,7},{10,8},{11,9},{8,1... | collective-permute-start | bytes 12582920 | tf_op jit(solution)/shard_map/ppermute | solution.py:283
  103.1 98.8 %collective-permute-start.9 = (f32[2,32,128,128]{3,2,1,0:T(8,128)}, f32[2,32,128,128]{3,2,1,0:T(8,128)}, u32[]{:S(2)}, u32[]{:S(2)}) collective-permute-start(f32[2,32,128,128]{3,2,1,0:T(8,128)} %collective-permute-done.7.refs_2_), channel_id=1, source_target_pairs={{2,0},{3,1},{0,2},{1,3},{6,4},{7,5},{4,6},{5,7},{10,8},{11,9},{8,1... | collective-permute-start | bytes 12582920 | tf_op jit(solution)/shard_map/ppermute | solution.py:283
  192.2 98.0 %collective-permute-start.5 = (f32[2,32,128,128]{3,2,1,0:T(8,128)}, f32[2,32,128,128]{3,2,1,0:T(8,128)}, u32[]{:S(2)}, u32[]{:S(2)}) collective-permute-start(f32[2,32,128,128]{3,2,1,0:T(8,128)} %collective-permute-done.3.refs_2_), channel_id=1, source_target_pairs={{2,0},{3,1},{0,2},{1,3},{6,4},{7,5},{4,6},{5,7},{10,8},{11,9},{8,1... | collective-permute-start | bytes 12582920 | tf_op jit(solution)/shard_map/ppermute | solution.py:283
  198.3 95.0 %collective-permute-start = (f32[2,32,128,128]{3,2,1,0:T(8,128)}, f32[2,32,128,128]{3,2,1,0:T(8,128)}, u32[]{:S(2)}, u32[]{:S(2)}) collective-permute-start(f32[2,32,128,128]{3,2,1,0:T(8,128)} %constant_dynamic-slice_fusion.4), channel_id=1, source_target_pairs={{1,0},{0,1},{3,2},{2,3},{5,4},{4,5},{7,6},{6,7},{9,8},{8,9},{11,10... | collective-permute-start | bytes 12582920 | tf_op jit(solution)/shard_map/ppermute | solution.py:289
  198.3 95.5 %collective-permute-start.2 = (f32[2,32,128,128]{3,2,1,0:T(8,128)}, f32[2,32,128,128]{3,2,1,0:T(8,128)}, u32[]{:S(2)}, u32[]{:S(2)}) collective-permute-start(f32[2,32,128,128]{3,2,1,0:T(8,128)} %collective-permute-done.1), channel_id=1, source_target_pairs={{1,0},{0,1},{3,2},{2,3},{5,4},{4,5},{7,6},{6,7},{9,8},{8,9},{11,10... | collective-permute-start | bytes 12582920 | tf_op jit(solution)/shard_map/ppermute | solution.py:289
  200.6 104.0 %collective-permute-start.8 = (f32[1,32,128,128]{3,2,1,0:T(8,128)S(1)}, f32[1,32,128,128]{3,2,1,0:T(8,128)S(1)}, u32[]{:S(2)}, u32[]{:S(2)}) collective-permute-start(f32[1,32,128,128]{3,2,1,0:T(8,128)S(1)} %constant_dynamic-slice_fusion.1), channel_id=1, source_target_pairs={{1,0},{0,1},{3,2},{2,3},{5,4},{4,5},{7,6},{6,7},{9,8},{8,9},{11,10... | collective-permute-start | bytes 6291464 | tf_op jit(solution)/shard_map/ppermute | solution.py:289
  203.7 100.9 %collective-permute-start.10 = (f32[1,32,128,128]{3,2,1,0:T(8,128)S(1)}, f32[1,32,128,128]{3,2,1,0:T(8,128)}, u32[]{:S(2)}, u32[]{:S(2)}) collective-permute-start(f32[1,32,128,128]{3,2,1,0:T(8,128)S(1)} %constant_dynamic-slice_fusion), channel_id=1, source_target_pairs={{1,0},{0,1},{3,2},{2,3},{5,4},{4,5},{7,6},{6,7},{9,8},{8,9},{11,10... | collective-permute-start | bytes 6291464 | tf_op jit(solution)/shard_map/ppermute | solution.py:289
  290.1 87.0 %collective-permute-start.4 = (f32[1,32,128,128]{3,2,1,0:T(8,128)}, f32[1,32,128,128]{3,2,1,0:T(8,128)}, u32[]{:S(2)}, u32[]{:S(2)}) collective-permute-start(f32[1,32,128,128]{3,2,1,0:T(8,128)} %constant_dynamic-slice_fusion.3), channel_id=1, source_target_pairs={{1,0},{0,1},{3,2},{2,3},{5,4},{4,5},{7,6},{6,7},{9,8},{8,9},{11,10... | collective-permute-start | bytes 6291464 | tf_op jit(solution)/shard_map/ppermute | solution.py:289
  293.3 83.8 %collective-permute-start.6 = (f32[1,32,128,128]{3,2,1,0:T(8,128)}, f32[1,32,128,128]{3,2,1,0:T(8,128)}, u32[]{:S(2)}, u32[]{:S(2)}) collective-permute-start(f32[1,32,128,128]{3,2,1,0:T(8,128)} %constant_dynamic-slice_fusion.2), channel_id=1, source_target_pairs={{1,0},{0,1},{3,2},{2,3},{5,4},{4,5},{7,6},{6,7},{9,8},{8,9},{11,10... | collective-permute-start | bytes 6291464 | tf_op jit(solution)/shard_map/ppermute | solution.py:289
  375.6 78.7 %collective-permute-start.15 = (f32[32,128,128]{2,1,0:T(8,128)}, f32[32,128,128]{2,1,0:T(8,128)S(1)}, u32[]{:S(2)}, u32[]{:S(2)}) collective-permute-start(f32[32,128,128]{2,1,0:T(8,128)} %get-tuple-element.24), channel_id=1, source_target_pairs={{2,0},{3,1},{0,2},{1,3},{6,4},{7,5},{4,6},{5,7},{10,8},{11,9},{8,1... | collective-permute-start | bytes 6291464 | tf_op jit(solution)/shard_map/ppermute | solution.py:283
  453.2 22.8 %collective-permute-start.11 = (f32[2,32,128,128]{3,2,1,0:T(8,128)S(1)}, f32[2,32,128,128]{3,2,1,0:T(8,128)}, u32[]{:S(2)}, u32[]{:S(2)}) collective-permute-start(f32[2,32,128,128]{3,2,1,0:T(8,128)S(1)} %get-tuple-element.37), channel_id=1, source_target_pairs={{1,0},{0,1},{3,2},{2,3},{5,4},{4,5},{7,6},{6,7},{9,8},{8,9},{11,10... | collective-permute-start | bytes 12582920 | tf_op jit(solution)/shard_map/ppermute | solution.py:289
  453.3 24.5 %collective-permute-start.12 = (f32[2,32,128,128]{3,2,1,0:T(8,128)S(1)}, f32[2,32,128,128]{3,2,1,0:T(8,128)S(1)}, u32[]{:S(2)}, u32[]{:S(2)}) collective-permute-start(f32[2,32,128,128]{3,2,1,0:T(8,128)S(1)} %get-tuple-element.36), channel_id=1, source_target_pairs={{1,0},{0,1},{3,2},{2,3},{5,4},{4,5},{7,6},{6,7},{9,8},{8,9},{11,10... | collective-permute-start | bytes 12582920 | tf_op jit(solution)/shard_map/ppermute | solution.py:289
  469.6 48.8 %collective-permute-start.19 = (f32[32,128,128]{2,1,0:T(8,128)}, f32[32,128,128]{2,1,0:T(8,128)}, u32[]{:S(2)}, u32[]{:S(2)}) collective-permute-start(f32[32,128,128]{2,1,0:T(8,128)} %collective-permute-done.18), channel_id=1, source_target_pairs={{2,0},{3,1},{0,2},{1,3},{6,4},{7,5},{4,6},{5,7},{10,8},{11,9},{8,1... | collective-permute-start | bytes 6291464 | tf_op jit(solution)/shard_map/ppermute | solution.py:283
  472.5 90.9 %collective-permute-start.21 = (f32[32,128,128]{2,1,0:T(8,128)}, f32[32,128,128]{2,1,0:T(8,128)}, u32[]{:S(2)}, u32[]{:S(2)}) collective-permute-start(f32[32,128,128]{2,1,0:T(8,128)} %get-tuple-element.29), channel_id=1, source_target_pairs={{2,0},{3,1},{0,2},{1,3},{6,4},{7,5},{4,6},{5,7},{10,8},{11,9},{8,1... | collective-permute-start | bytes 6291464 | tf_op jit(solution)/shard_map/ppermute | solution.py:283
  475.6 132.7 %collective-permute-start.25 = (f32[32,128,128]{2,1,0:T(8,128)}, f32[32,128,128]{2,1,0:T(8,128)}, u32[]{:S(2)}, u32[]{:S(2)}) collective-permute-start(f32[32,128,128]{2,1,0:T(8,128)} %collective-permute-done.24), channel_id=1, source_target_pairs={{2,0},{3,1},{0,2},{1,3},{6,4},{7,5},{4,6},{5,7},{10,8},{11,9},{8,1... | collective-permute-start | bytes 6291464 | tf_op jit(solution)/shard_map/ppermute | solution.py:283
  476.0 135.5 %collective-permute-start.23 = (f32[32,128,128]{2,1,0:T(8,128)}, f32[32,128,128]{2,1,0:T(8,128)}, u32[]{:S(2)}, u32[]{:S(2)}) collective-permute-start(f32[32,128,128]{2,1,0:T(8,128)} %get-tuple-element.31), channel_id=1, source_target_pairs={{1,0},{0,1},{3,2},{2,3},{5,4},{4,5},{7,6},{6,7},{9,8},{8,9},{11,10... | collective-permute-start | bytes 6291464 | tf_op jit(solution)/shard_map/ppermute | solution.py:289
  479.8 136.2 %collective-permute-start.16 = (f32[32,128,128]{2,1,0:T(8,128)}, f32[32,128,128]{2,1,0:T(8,128)}, u32[]{:S(2)}, u32[]{:S(2)}) collective-permute-start(f32[32,128,128]{2,1,0:T(8,128)} %add.94), channel_id=1, source_target_pairs={{4,0},{8,4},{12,8},{16,12},{20,16},{24,20},{28,24},{0,28},{5,1},{9... | collective-permute-start | bytes 6291464 | tf_op jit(solution)/shard_map/ppermute | solution.py:294
  518.4 134.8 %collective-permute-start.13 = (f32[1,32,128,128]{3,2,1,0:T(8,128)}, f32[1,32,128,128]{3,2,1,0:T(8,128)}, u32[]{:S(2)}, u32[]{:S(2)}) collective-permute-start(f32[1,32,128,128]{3,2,1,0:T(8,128)} %get-tuple-element.39), channel_id=1, source_target_pairs={{2,0},{3,1},{0,2},{1,3},{6,4},{7,5},{4,6},{5,7},{10,8},{11,9},{8,1... | collective-permute-start | bytes 6291464 | tf_op jit(solution)/shard_map/ppermute | solution.py:283
  563.4 91.7 %collective-permute-start.20 = (f32[32,128,128]{2,1,0:T(8,128)S(1)}, f32[32,128,128]{2,1,0:T(8,128)}, u32[]{:S(2)}, u32[]{:S(2)}) collective-permute-start(f32[32,128,128]{2,1,0:T(8,128)S(1)} %add.97), channel_id=1, source_target_pairs={{4,0},{8,4},{12,8},{16,12},{20,16},{24,20},{28,24},{0,28},{5,1},{9... | collective-permute-start | bytes 6291464 | tf_op jit(solution)/shard_map/ppermute | solution.py:294
  608.3 49.5 %collective-permute-start.22 = (f32[32,128,128]{2,1,0:T(8,128)}, f32[32,128,128]{2,1,0:T(8,128)}, u32[]{:S(2)}, u32[]{:S(2)}) collective-permute-start(f32[32,128,128]{2,1,0:T(8,128)} %add.99), channel_id=1, source_target_pairs={{4,0},{8,4},{12,8},{16,12},{20,16},{24,20},{28,24},{0,28},{5,1},{9... | collective-permute-start | bytes 6291464 | tf_op jit(solution)/shard_map/ppermute | solution.py:294
  615.4 84.8 %collective-permute-start.26 = (f32[32,128,128]{2,1,0:T(8,128)}, f32[32,128,128]{2,1,0:T(8,128)}, u32[]{:S(2)}, u32[]{:S(2)}) collective-permute-start(f32[32,128,128]{2,1,0:T(8,128)} %add.102), channel_id=1, source_target_pairs={{4,0},{8,4},{12,8},{16,12},{20,16},{24,20},{28,24},{0,28},{5,1},{9... | collective-permute-start | bytes 6291464 | tf_op jit(solution)/shard_map/ppermute | solution.py:294
  616.0 86.0 %collective-permute-start.14 = (f32[1,32,128,128]{3,2,1,0:T(8,128)}, f32[1,32,128,128]{3,2,1,0:T(8,128)}, u32[]{:S(2)}, u32[]{:S(2)}) collective-permute-start(f32[1,32,128,128]{3,2,1,0:T(8,128)} %get-tuple-element.38), channel_id=1, source_target_pairs={{2,0},{3,1},{0,2},{1,3},{6,4},{7,5},{4,6},{5,7},{10,8},{11,9},{8,1... | collective-permute-start | bytes 6291464 | tf_op jit(solution)/shard_map/ppermute | solution.py:283
  (14 other events, 211.0 us)
